TPU v7x, 32 devices: a whole 2x2x4 slice. The times are simulated.
32 devices in a mesh: det: 4 (over y, x), tm: 8 (over z, core).
Axes of the slice: x: 2, y: 2, z: 4, core: 2. Of those that a mesh axis runs over, the one named last changes fastest.
Arguments:
- sol_map: float32 [3, 49152], P(None, ('det', 'tm')), may hold values from -6 to 6
- resid_map: float32 [3, 49152], P(None, ('det', 'tm')), may hold values from -6 to 6
- direction: float32 [3, 49152], P(None, ('det', 'tm')), may hold values from -6 to 6
- precond: float32 [3, 49152], P(None, ('det', 'tm')), may hold values from 0.1 to 1
- pixels: int32 [128, 65536], P('det', 'tm'), may hold values from 0 to 49151
- angle_index: int32 [128, 65536], P('det', 'tm'), may hold values from 0 to 127
- angles: float32 [128], replicated, may hold values from -3.140625 to 3.140625
- flag_mask: int32 [128, 65536], P('det', 'tm'), may hold values 0 or 1
- inv_noise: float32 [128, 32769], P(('det', 'tm')), may hold values from 0.05 to 1
Outputs:
- new_sol: float32 [3, 49152], P(None, ('det', 'tm'))
- new_resid: float32 [3, 49152], P(None, ('det', 'tm'))
- new_dir: float32 [3, 49152], P(None, ('det', 'tm'))
- new_norm: float32 [], replicated
All inputs are finite; a program needn't handle non-finite values. No bound on the sum of `flag_mask` on one device may be relied on, other than what follows from the above.
Results may differ from a plain program's by a relative error of at most 0.0001.
Values sent between devices are 32-bit elements; how exact they have to be, the bound alone decides.
A program may use at most 320 MiB of HBM per device.

v0:
```python
import functools
import math

import jax
import jax.numpy as jnp
from jax import lax
from jax.experimental import pallas as pl
from jax.experimental.pallas import tpu as pltpu
from jax.sharding import PartitionSpec as P

LOW = 256
ROWS = 8
PACK = 16
LANES = 128
WIDTH = 512


def product(form, left, right, precision=lax.Precision.HIGH):
    return jnp.einsum(form, left, right, precision=precision)


def split_two(values):
    upper = values.astype(jnp.bfloat16)
    lower = (values - upper.astype(jnp.float32)).astype(jnp.bfloat16)
    return upper, lower


def lookup(table_row, index):
    rows, width = index.shape
    table = jnp.broadcast_to(table_row, (rows, LANES))
    parts = []
    for start in range(0, width, LANES):
        parts.append(jnp.take_along_axis(table, index[:, start : start + LANES], axis=1, mode="promise_in_bounds"))
    return jnp.concatenate(parts, axis=1)


def one_hot(row, size):
    ids = lax.broadcasted_iota(jnp.int32, (size, row.shape[1]), 0)
    return jnp.where(ids == row, 1.0, 0.0).astype(jnp.bfloat16)


def read_kernel(trig_ref, table_ref, pix_ref, ang_ref, flag_ref, out_ref, split_ref, *, high):
    @pl.when(pl.program_id(0) * pl.num_programs(1) + pl.program_id(1) == 0)
    def _():
        upper, lower = split_two(table_ref[...])
        split_ref[:, :LOW] = upper
        split_ref[:, LOW:] = lower

    cos_two = lookup(trig_ref[0:1, :], ang_ref[...])
    sin_two = lookup(trig_ref[1:2, :], ang_ref[...])
    usable = flag_ref[...].astype(jnp.float32)
    pix = pix_ref[...]
    pix_low = pix & (LOW - 1)
    pix_high = pix // LOW if LOW & (LOW - 1) else pix >> (LOW.bit_length() - 1)
    width = pix.shape[1]
    ids = lax.broadcasted_iota(jnp.int32, (high, width), 0)
    for row in range(ROWS):
        hot = one_hot(pix_low[row : row + 1], LOW)
        got = jnp.dot(split_ref[...], jnp.concatenate([hot, hot], axis=0), preferred_element_type=jnp.float32)
        mixed = got[:high] + got[high : 2 * high] * cos_two[row : row + 1] + got[2 * high :] * sin_two[row : row + 1]
        picked = jnp.sum(jnp.where(ids == pix_high[row : row + 1], mixed, 0.0), axis=0, keepdims=True)
        out_ref[row : row + 1, :] = picked * usable[row : row + 1]


def bin_kernel(trig_ref, pix_ref, ang_ref, flag_ref, val_ref, out_ref, *, high):
    step = pl.program_id(0) * pl.num_programs(1) + pl.program_id(1)

    @pl.when(step == 0)
    def _():
        out_ref[...] = jnp.zeros_like(out_ref)

    cos_two = lookup(trig_ref[0:1, :], ang_ref[...])
    sin_two = lookup(trig_ref[1:2, :], ang_ref[...])
    weighted = flag_ref[...].astype(jnp.float32) * val_ref[...]
    pieces = []
    for stokes in (weighted, weighted * cos_two, weighted * sin_two):
        upper = stokes.astype(jnp.bfloat16).astype(jnp.float32)
        pieces.append((upper, stokes - upper))
    pix = pix_ref[...]
    pix_low = pix & (LOW - 1)
    pix_high = pix >> (LOW.bit_length() - 1)
    total = None
    for row in range(ROWS):
        hot_low = one_hot(pix_low[row : row + 1], LOW)
        hot_high = one_hot(pix_high[row : row + 1], high)
        hot_high = hot_high.reshape(high // PACK, PACK, hot_high.shape[1])
        stack = []
        for part in range(2):
            for stokes in range(3):
                value = pieces[stokes][part][row : row + 1]
                value = jnp.broadcast_to(value, (PACK, value.shape[1])).astype(jnp.bfloat16)
                stack.append((hot_high * value[None]).reshape(high, value.shape[1]))
        left = jnp.concatenate(stack, axis=0)
        got = lax.dot_general(left, hot_low, (((1,), (1,)), ((), ())), preferred_element_type=jnp.float32)
        total = got if total is None else total + got
    out_ref[...] += total


def read_map(trig, table, pixels, angle_index, flag_mask):
    n_det, n_samp = pixels.shape
    high = table.shape[0] // 3
    block = pl.BlockSpec((ROWS, WIDTH), lambda i, j: (i, j))
    fixed = lambda shape: pl.BlockSpec(shape, lambda i, j: (0, 0))
    return pl.pallas_call(
        functools.partial(read_kernel, high=high),
        out_shape=jax.ShapeDtypeStruct((n_det, n_samp), jnp.float32),
        grid=(n_det // ROWS, n_samp // WIDTH),
        in_specs=[fixed(trig.shape), fixed(table.shape), block, block, block],
        out_specs=block,
        scratch_shapes=[pltpu.VMEM((3 * high, 2 * LOW), jnp.bfloat16)],
        compiler_params=pltpu.CompilerParams(dimension_semantics=("arbitrary", "arbitrary")),
        name="read_map",
    )(trig, table, pixels, angle_index, flag_mask)


def bin_map(trig, pixels, angle_index, flag_mask, values, high):
    n_det, n_samp = pixels.shape
    block = pl.BlockSpec((ROWS, WIDTH), lambda i, j: (i, j))
    fixed = lambda shape: pl.BlockSpec(shape, lambda i, j: (0, 0))
    pieces = pl.pallas_call(
        functools.partial(bin_kernel, high=high),
        out_shape=jax.ShapeDtypeStruct((6 * high, LOW), jnp.float32),
        grid=(n_det // ROWS, n_samp // WIDTH),
        in_specs=[fixed(trig.shape), block, block, block, block],
        out_specs=fixed((6 * high, LOW)),
        compiler_params=pltpu.CompilerParams(dimension_semantics=("arbitrary", "arbitrary")),
        name="bin_map",
    )(trig, pixels, angle_index, flag_mask, values)
    return pieces[: 3 * high] + pieces[3 * high :]


def mirrored(filt, side_len):
    n_series, half_len = filt.shape
    rows = (half_len - 1) // side_len
    lower = filt[:, : half_len - 1].reshape(n_series, rows, side_len)
    shifted = filt[:, 1:].reshape(n_series, rows, side_len)
    swap_col = jnp.flip(jnp.eye(side_len, dtype=jnp.float32), 0)
    swap_row = jnp.flip(jnp.eye(rows, dtype=jnp.float32), 0)
    exact = lax.Precision.HIGHEST
    upper = product("wv,dvk->dwk", swap_row, product("dvk,kl->dvl", shifted, swap_col, exact), exact)
    return jnp.concatenate([lower, upper], axis=1)


def noise_weight(series, filt):
    n_series, total_len = series.shape
    side_len = math.isqrt(total_len)
    indices = jnp.arange(side_len, dtype=jnp.int32)
    products = indices[:, None] * indices[None, :]
    angle_tab = 2.0 * math.pi / side_len * (products % side_len).astype(jnp.float32)
    f_real = jnp.cos(angle_tab)
    f_imag = -jnp.sin(angle_tab)
    twist = products.astype(jnp.float32) * (2.0 * math.pi / total_len)
    w_real = jnp.cos(twist)
    w_imag = -jnp.sin(twist)
    matrix_form = series.reshape(n_series, side_len, side_len)
    y_real = product("kt,dtu->dku", f_real, matrix_form)
    y_imag = product("kt,dtu->dku", f_imag, matrix_form)
    y_real, y_imag = (y_real * w_real - y_imag * w_imag, y_real * w_imag + y_imag * w_real)
    z_real = product("dku,uv->dvk", y_real, f_real) - product("dku,uv->dvk", y_imag, f_imag)
    z_imag = product("dku,uv->dvk", y_real, f_imag) + product("dku,uv->dvk", y_imag, f_real)
    weight = mirrored(filt, side_len)
    z_real = z_real * weight
    z_imag = z_imag * weight
    v_real = product("dvk,vu->dku", z_real, f_real) + product("dvk,vu->dku", z_imag, f_imag)
    v_imag = product("dvk,vu->dku", z_imag, f_real) - product("dvk,vu->dku", z_real, f_imag)
    v_real, v_imag = (v_real * w_real + v_imag * w_imag, v_imag * w_real - v_real * w_imag)
    result = product("tk,dku->dtu", f_real, v_real) + product("tk,dku->dtu", f_imag, v_imag)
    return (result / total_len).reshape(n_series, total_len)


def body(sol_map, resid_map, direction, precond, pixels, angle_index, angles, flag_mask, inv_noise):
    everyone = ("det", "tm")
    share_len = direction.shape[1]
    n_dev = lax.axis_size(everyone)
    copies = jnp.broadcast_to(direction.reshape(1, -1, LANES), (n_dev, direction.size // LANES, LANES))
    gathered = lax.all_to_all(copies, everyone, split_axis=0, concat_axis=0, tiled=True)
    high = n_dev * share_len // LOW
    table = jnp.swapaxes(gathered.reshape(n_dev, 3, share_len), 0, 1).reshape(3 * high, LOW)
    trig = jnp.stack([jnp.cos(2.0 * angles), jnp.sin(2.0 * angles)])
    signal = read_map(trig, table, pixels, angle_index, flag_mask)
    by_detector = lax.all_to_all(signal, "tm", split_axis=0, concat_axis=1, tiled=True)
    filtered = noise_weight(by_detector, inv_noise)
    returned = lax.all_to_all(filtered, "tm", split_axis=1, concat_axis=0, tiled=True)
    partial_map = bin_map(trig, pixels, angle_index, flag_mask, returned, high)
    by_owner = jnp.swapaxes(partial_map.reshape(3, n_dev, share_len), 0, 1)
    image = jnp.sum(lax.all_to_all(by_owner, everyone, split_axis=0, concat_axis=0, tiled=True), axis=0)
    scaled_resid = precond * resid_map
    own_sums = jnp.stack(
        [
            jnp.sum(scaled_resid * resid_map),
            jnp.sum(direction * image),
            jnp.sum(image * scaled_resid),
            jnp.sum(image * precond * image),
        ]
    )
    sum_copies = jnp.broadcast_to(own_sums[None], (n_dev, own_sums.shape[0]))
    all_sums = lax.all_to_all(sum_copies, everyone, split_axis=0, concat_axis=0, tiled=True)
    norm_old, curvature, cross_term, image_norm = jnp.sum(all_sums, axis=0)
    step_size = norm_old / curvature
    new_resid = resid_map - step_size * image
    new_norm = norm_old - 2.0 * step_size * cross_term + step_size * step_size * image_norm
    new_sol = sol_map + step_size * direction
    new_dir = precond * new_resid + new_norm / norm_old * direction
    return (new_sol, new_resid, new_dir, new_norm)


def solution(mesh):
    in_specs = (
        P(None, ("det", "tm")),
        P(None, ("det", "tm")),
        P(None, ("det", "tm")),
        P(None, ("det", "tm")),
        P("det", "tm"),
        P("det", "tm"),
        P(),
        P("det", "tm"),
        P(("det", "tm"), None),
    )
    out_specs = (P(None, ("det", "tm")), P(None, ("det", "tm")), P(None, ("det", "tm")), P())
    return jax.shard_map(body, mesh=mesh, in_specs=in_specs, out_specs=out_specs, check_vma=False)
```

profile of v0, /device:TPU:0, one launch (start us, length us, event | category | flops | bytes accessed | tf_op | source)
XLA Modules:
  0.0 526.6 jit_solution(11339445354091524032)
XLA Ops:
  0.6 0.8 broadcast_in_dim.6
  1.4 0.9 broadcast_in_dim.7
  2.3 7.3 %all-to-all-start = ((f32[32,36,128]{2,1,0:T(8,128)}), f32[32,36,128]{2,1,0:T(8,128)S(1)}, u32[]{:S(2)}, u32[]{:S(2)}) async-start(f32[32,36,128]{2,1,0:T(8,128)} %broadcast_in_dim.7), calls=%async_computation | async-start | bytes 1310720 | tf_op jit(solution)/shard_map/all_to_all | solution.py:176
  9.7 0.6 pad_maximum_fusion.1.trig_ref
  10.2 18.4 %all-to-all-done = f32[32,36,128]{2,1,0:T(8,128)S(1)} async-done(((f32[32,36,128]{2,1,0:T(8,128)}), f32[32,36,128]{2,1,0:T(8,128)S(1)}, u32[]{:S(2)}, u32[]{:S(2)}) %all-to-all-start) | async-done | bytes 589856 | tf_op jit(solution)/shard_map/all_to_all | solution.py:176
  28.7 0.2 reshape.69
  28.9 0.2 copy.107
  29.1 1.0 reshape.70.table_ref
  30.0 188.4 %read_map.1 = f32[32,8192]{1,0:T(8,128)} custom-call(f32[2,128]{1,0:T(2,128)} %pad_maximum_fusion.1.trig_ref, f32[576,256]{1,0:T(8,128)} %reshape.70.table_ref, s32[32,8192]{1,0:T(8,128)} %pix_ref.3, s32[32,8192]{1,0:T(8,128)} %ang_ref.3, s32[32,8192]{1,0:T(8,128)} %flag_ref.3), custom_call_target="tpu_custom_call" | custom-call | tf_op jit(solution)/shard_map/read_map/pallas_call | solution.py:104
  218.5 2.6 all_to_all.37
  221.0 3.6 all-to-all-start.1
  224.6 1.6 fusion.102
  226.2 0.5 rev.8
  226.8 0.9 fusion.39
  227.8 0.9 sine_negate_fusion
  228.9 0.7 convolution_bitcast_fusion.3
  229.6 0.6 convolution_bitcast_fusion.2
  230.2 20.9 %all-to-all-done.1 = f32[8,4,8192]{2,1,0:T(4,128)S(1)} async-done(((f32[8,4,8192]{2,1,0:T(4,128)}), f32[8,4,8192]{2,1,0:T(4,128)S(1)}, u32[]{:S(2)}, u32[]{:S(2)}) %all-to-all-start.1) | async-done | bytes 1048608 | tf_op jit(solution)/shard_map/all_to_all | solution.py:181
  251.1 1.6 copy.108
  252.7 1.4 reshape.71
  254.1 1.8 convolution_bitcast_fusion
  255.9 1.8 convolution_bitcast_fusion.1
  257.7 1.7 fusion.23
  259.4 1.7 fusion.37
  261.0 2.0 fusion.3
  263.0 1.7 fusion.5
  264.7 1.6 fusion.34
  266.3 1.6 fusion.32
  267.9 1.6 convolution_add_fusion.1
  269.5 1.6 convolution_subtract_fusion
  271.1 1.6 fusion.9
  272.8 1.9 fusion.1
  274.7 0.3 copy.130
  275.1 0.2 all_to_all.40
  275.3 0.7 copy.131
  276.0 29.0 %all_to_all.51 = f32[4,8,8192]{2,0,1:T(4,128)S(1)} all-to-all(f32[4,8,8192]{2,0,1:T(4,128)S(1)} %copy.131), channel_id=1, replica_groups=mesh['det'=4,'tm'=8] {'tm'}, dimensions={1} | all-to-all | bytes 2097152 | tf_op jit(solution)/shard_map/all_to_all | solution.py:183
  305.0 1.4 all_to_all.43.val_ref
  306.3 175.7 %bin_map.1 = f32[1152,256]{1,0:T(8,128)} custom-call(f32[2,128]{1,0:T(2,128)} %pad_maximum_fusion.1.trig_ref, s32[32,8192]{1,0:T(8,128)} %pix_ref.3, s32[32,8192]{1,0:T(8,128)} %ang_ref.3, s32[32,8192]{1,0:T(8,128)} %flag_ref.3, f32[32,8192]{1,0:T(8,128)} %all_to_all.43.val_ref), custom_call_target="tpu_custom_call" | custom-call | tf_op jit(solution)/shard_map/bin_map/pallas_call | solution.py:120
  482.0 1.3 slice_add_fusion
  483.3 0.2 reshape.74
  483.5 0.4 copy.170
  484.0 23.6 %all_to_all.52 = f32[32,3,1536]{2,1,0:T(4,128)S(1)} all-to-all(f32[32,3,1536]{2,1,0:T(4,128)S(1)} %bitcast.91), channel_id=1, replica_groups=mesh['det'=4,'tm'=8] {'det','tm'}, dimensions={0} | all-to-all | bytes 1179648 | tf_op jit(solution)/shard_map/all_to_all | solution.py:186
  507.6 0.1 reduce_sum.55
  507.7 0.6 multiply_reduce_fusion.2
  508.3 2.7 pad_maximum_fusion.2
  511.0 9.2 %all_to_all.53 = f32[32,1,4]{2,1,0:T(1,128)S(1)} all-to-all(f32[32,1,4]{2,1,0:T(1,128)S(1)} %broadcast_in_dim.8), channel_id=1, replica_groups=mesh['det'=4,'tm'=8] {'det','tm'}, dimensions={0} | all-to-all | bytes 1024 | tf_op jit(solution)/shard_map/all_to_all | solution.py:197
  520.3 0.6 fusion.103
  524.8 0.6 multiply_add_fusion.3
  (19 shorter events, 0.5 us)
Async XLA Ops:
  0.6 9.0 %copy-start.4 = (f32[128]{0:T(128)S(1)}, f32[128]{0:T(128)}, u32[]{:S(2)}) copy-start(f32[128]{0:T(128)} %param.15) | copy-start | bytes 1540
  2.3 26.4 %all-to-all-start = ((f32[32,36,128]{2,1,0:T(8,128)}), f32[32,36,128]{2,1,0:T(8,128)S(1)}, u32[]{:S(2)}, u32[]{:S(2)}) async-start(f32[32,36,128]{2,1,0:T(8,128)} %broadcast_in_dim.7), calls=%async_computation | async-start | bytes 1310720 | tf_op jit(solution)/shard_map/all_to_all | solution.py:176
  221.0 30.1 %all-to-all-start.1 = ((f32[8,4,8192]{2,1,0:T(4,128)}), f32[8,4,8192]{2,1,0:T(4,128)S(1)}, u32[]{:S(2)}, u32[]{:S(2)}) async-start(f32[8,4,8192]{2,1,0:T(4,128)} %all_to_all.37), calls=%async_computation.1 | async-start | bytes 2097152 | tf_op jit(solution)/shard_map/all_to_all | solution.py:181
  483.9 23.8 %copy-start = (f32[3,1536]{1,0:T(4,128)S(1)}, f32[3,1536]{1,0:T(4,128)}, u32[]{:S(2)}) copy-start(f32[3,1536]{1,0:T(4,128)} %param.11) | copy-start | bytes 55300
  483.9 23.8 %copy-start.1 = (f32[3,1536]{1,0:T(4,128)S(1)}, f32[3,1536]{1,0:T(4,128)}, u32[]{:S(2)}) copy-start(f32[3,1536]{1,0:T(4,128)} %param.12) | copy-start | bytes 55300
  484.0 23.8 %copy-start.2 = (f32[3,1536]{1,0:T(4,128)S(1)}, f32[3,1536]{1,0:T(4,128)}, u32[]{:S(2)}) copy-start(f32[3,1536]{1,0:T(4,128)} %param.10) | copy-start | bytes 55300
  484.0 40.9 %copy-start.3 = (f32[3,1536]{1,0:T(4,128)S(1)}, f32[3,1536]{1,0:T(4,128)}, u32[]{:S(2)}) copy-start(f32[3,1536]{1,0:T(4,128)} %param.9) | copy-start | bytes 55300
where the time goes:
time: 527 us
  Pallas kernels  364 us (69%)
  blocking collectives  61.8 us (12%)
  waiting for transfers between devices  39.3 us (7%)
  matrix products  21.9 us (4%)
  local copies, waits for them, and re-layouts  14.8 us (3%)
  starting transfers between devices  10.9 us (2%)
  other arithmetic  7.84 us (1%)
  between operations  6.04 us (1%)
    pallas_call x1, Pallas kernels, read_map(): pl.pallas_call(functools.partial(read_kernel, high=high), out_shape=jax.S...  188 us
    pallas_call x1, Pallas kernels, bin_map(): pl.pallas_call(functools.partial(bin_kernel, high=high), out_shape=jax.Sh...  176 us
    all_to_all x1, blocking collectives, body(): lax.all_to_all(filtered, 'tm', split_axis=1, concat_axis=0, tiled=True)  29 us
    all_to_all x1, blocking collectives, body(): lax.all_to_all(by_owner, everyone, split_axis=0, concat_axis=0, tiled=True)  23.6 us
    dot_general x14, matrix products, product(): return jnp.einsum(form, left, right, precision=precision)  21.9 us
    all_to_all x1, waiting for transfers between devices, body(): lax.all_to_all(signal, 'tm', split_axis=0, concat_axis=1, tiled=True)  20.9 us
    all_to_all x1, waiting for transfers between devices, body(): lax.all_to_all(copies, everyone, split_axis=0, concat_axis=0, tiled=True)  18.4 us
  transfers between devices with their start and end apart: 2, of which 2 were waited for; matrix products, arithmetic and copies ran while one was open for 1% of the time, Pallas kernels for 0%

commit v1 on v0

--- a/solution.py
+++ b/solution.py
@@ -10,19 +10,18 @@
 
 LOW = 256
 ROWS = 8
-PACK = 16
 LANES = 128
-WIDTH = 512
+WIDTH = 1024
+CHUNKS = 2
+CHUNKS_BACK = 1
+TOP = 400.0
+STEP = 16.0
+F8 = jnp.float8_e4m3fn
+BF16 = jnp.bfloat16
 
 
 def product(form, left, right, precision=lax.Precision.HIGH):
     return jnp.einsum(form, left, right, precision=precision)
-
-
-def split_two(values):
-    upper = values.astype(jnp.bfloat16)
-    lower = (values - upper.astype(jnp.float32)).astype(jnp.bfloat16)
-    return upper, lower
 
 
 def lookup(table_row, index):
@@ -34,99 +33,182 @@
     return jnp.concatenate(parts, axis=1)
 
 
-def one_hot(row, size):
-    ids = lax.broadcasted_iota(jnp.int32, (size, row.shape[1]), 0)
-    return jnp.where(ids == row, 1.0, 0.0).astype(jnp.bfloat16)
-
-
-def read_kernel(trig_ref, table_ref, pix_ref, ang_ref, flag_ref, out_ref, split_ref, *, high):
+def scale_of(values):
+    return TOP / jnp.maximum(jnp.max(jnp.abs(values)), 1e-30)
+
+
+def three_pieces(values):
+    first = values.astype(F8).astype(jnp.float32)
+    rest = values - first
+    second = rest.astype(F8).astype(jnp.float32)
+    return first, second, (rest - second) * STEP
+
+
+def wide_row(row, rows, dtype):
+    row = jnp.broadcast_to(row, (rows, row.shape[1]))
+    return row.astype(jnp.float32).astype(dtype)
+
+
+def select_tree(parts, bits):
+    level = 0
+    while len(parts) > 1:
+        pairs = [jnp.where(bits[level], parts[i + 1], parts[i]) for i in range(0, len(parts) - 1, 2)]
+        if len(parts) % 2:
+            pairs.append(parts[-1])
+        parts = pairs
+        level += 1
+    return parts[0]
+
+
+def hot_pair(row, size):
+    width = row.shape[1]
+    ids = wide_row(lax.broadcasted_iota(jnp.int32, (16, width), 0), 16, BF16)
+    same = wide_row(row & 15, 16, BF16) == ids
+    group = wide_row(row >> 4, 16, BF16)
+    zero = jnp.zeros((16, width), BF16)
+    out = []
+    for level in (1.0, 1.0 / STEP):
+        base = jnp.where(same, jnp.full((16, width), level, BF16), zero)
+        parts = [jnp.where(group == BF16(k), base, zero) for k in range(size // 16)]
+        out.append(jnp.concatenate(parts, axis=0).astype(F8))
+    return out
+
+
+def hot_pair_8(row, size):
+    width = row.shape[1]
+    ids = lax.broadcasted_iota(jnp.int32, (32, width), 0).astype(jnp.int8)
+    same = jnp.broadcast_to(row & 31, (32, width)).astype(jnp.int8) == ids
+    group = jnp.broadcast_to(row >> 5, (32, width)).astype(jnp.int8)
+    zero = jnp.zeros((32, width), F8)
+    masks = [group == jnp.int8(k) for k in range(size // 32)]
+    out = []
+    for level in (1.0, 1.0 / STEP):
+        base = jnp.where(same, jnp.full((32, width), level, F8), zero)
+        out.append(jnp.concatenate([jnp.where(mask, base, zero) for mask in masks], axis=0))
+    return out
+
+
+def read_kernel(trig_ref, table_ref, pix_ref, ang_ref, flag_ref, out_ref, split_ref, scale_ref, *, high):
     @pl.when(pl.program_id(0) * pl.num_programs(1) + pl.program_id(1) == 0)
     def _():
-        upper, lower = split_two(table_ref[...])
-        split_ref[:, :LOW] = upper
-        split_ref[:, LOW:] = lower
+        table = table_ref[...]
+        scale = scale_of(table)
+        scale_ref[0] = 1.0 / scale
+        for k, piece in enumerate(three_pieces(table * scale)):
+            split_ref[:, k * LOW : (k + 1) * LOW] = piece.astype(F8)
 
     cos_two = lookup(trig_ref[0:1, :], ang_ref[...])
     sin_two = lookup(trig_ref[1:2, :], ang_ref[...])
-    usable = flag_ref[...].astype(jnp.float32)
-    pix = pix_ref[...]
-    pix_low = pix & (LOW - 1)
-    pix_high = pix // LOW if LOW & (LOW - 1) else pix >> (LOW.bit_length() - 1)
-    width = pix.shape[1]
-    ids = lax.broadcasted_iota(jnp.int32, (high, width), 0)
-    for row in range(ROWS):
-        hot = one_hot(pix_low[row : row + 1], LOW)
-        got = jnp.dot(split_ref[...], jnp.concatenate([hot, hot], axis=0), preferred_element_type=jnp.float32)
-        mixed = got[:high] + got[high : 2 * high] * cos_two[row : row + 1] + got[2 * high :] * sin_two[row : row + 1]
-        picked = jnp.sum(jnp.where(ids == pix_high[row : row + 1], mixed, 0.0), axis=0, keepdims=True)
-        out_ref[row : row + 1, :] = picked * usable[row : row + 1]
-
-
-def bin_kernel(trig_ref, pix_ref, ang_ref, flag_ref, val_ref, out_ref, *, high):
-    step = pl.program_id(0) * pl.num_programs(1) + pl.program_id(1)
-
-    @pl.when(step == 0)
-    def _():
-        out_ref[...] = jnp.zeros_like(out_ref)
-
-    cos_two = lookup(trig_ref[0:1, :], ang_ref[...])
-    sin_two = lookup(trig_ref[1:2, :], ang_ref[...])
-    weighted = flag_ref[...].astype(jnp.float32) * val_ref[...]
-    pieces = []
-    for stokes in (weighted, weighted * cos_two, weighted * sin_two):
-        upper = stokes.astype(jnp.bfloat16).astype(jnp.float32)
-        pieces.append((upper, stokes - upper))
+    usable = flag_ref[...].astype(jnp.float32) * scale_ref[0]
     pix = pix_ref[...]
     pix_low = pix & (LOW - 1)
     pix_high = pix >> (LOW.bit_length() - 1)
+    width = pix.shape[1]
+    ids = lax.broadcasted_iota(jnp.int32, (8, width), 0)
+    count = high // 8
+    for row in range(ROWS):
+        one, small = hot_pair(pix_low[row : row + 1], LOW)
+        hot = jnp.concatenate([one, one, small], axis=0)
+        got = jnp.dot(split_ref[...], hot, preferred_element_type=jnp.float32)
+        upper = jnp.broadcast_to(pix_high[row : row + 1], (8, width))
+        bits = [(upper & (8 << level)) != 0 for level in range((count - 1).bit_length())]
+        picks = []
+        for stokes in range(3):
+            start = stokes * high
+            picks.append(select_tree([got[start + 8 * k : start + 8 * k + 8] for k in range(count)], bits))
+        mixed = picks[0] + picks[1] * cos_two[row : row + 1] + picks[2] * sin_two[row : row + 1]
+        picked = jnp.sum(jnp.where(ids == (upper & 7), mixed, 0.0), axis=0, keepdims=True)
+        out_ref[row : row + 1, :] = picked * usable[row : row + 1]
+
+
+def bin_kernel(trig_ref, scale_ref, pix_ref, ang_ref, flag_ref, val_ref, out_ref, *, high):
+    @pl.when(pl.program_id(0) * pl.num_programs(1) + pl.program_id(1) == 0)
+    def _():
+        out_ref[...] = jnp.zeros_like(out_ref)
+
+    cos_two = lookup(trig_ref[0:1, :], ang_ref[...])
+    sin_two = lookup(trig_ref[1:2, :], ang_ref[...])
+    weighted = flag_ref[...].astype(jnp.float32) * (val_ref[...] * scale_ref[0])
+    pieces = [three_pieces(stokes) for stokes in (weighted, weighted * cos_two, weighted * sin_two)]
+    pix = pix_ref[...]
+    pix_low = pix & (LOW - 1)
+    pix_high = pix >> (LOW.bit_length() - 1)
+    width = pix.shape[1]
+    ids = lax.broadcasted_iota(jnp.int32, (32, width), 0).astype(jnp.int8)
+    zero = jnp.zeros((32, width), F8)
     total = None
     for row in range(ROWS):
-        hot_low = one_hot(pix_low[row : row + 1], LOW)
-        hot_high = one_hot(pix_high[row : row + 1], high)
-        hot_high = hot_high.reshape(high // PACK, PACK, hot_high.shape[1])
-        stack = []
-        for part in range(2):
+        one, small = hot_pair_8(pix_low[row : row + 1], LOW)
+        upper = pix_high[row : row + 1]
+        same = jnp.broadcast_to(upper & 31, (32, width)).astype(jnp.int8) == ids
+        group = jnp.broadcast_to(upper >> 5, (32, width)).astype(jnp.int8)
+        masks = [group == jnp.int8(k) for k in range(high // 32)]
+        columns = []
+        for part in range(3):
+            stack = []
             for stokes in range(3):
                 value = pieces[stokes][part][row : row + 1]
-                value = jnp.broadcast_to(value, (PACK, value.shape[1])).astype(jnp.bfloat16)
-                stack.append((hot_high * value[None]).reshape(high, value.shape[1]))
-        left = jnp.concatenate(stack, axis=0)
-        got = lax.dot_general(left, hot_low, (((1,), (1,)), ((), ())), preferred_element_type=jnp.float32)
+                base = jnp.where(same, jnp.broadcast_to(value, (32, width)).astype(F8), zero)
+                stack += [jnp.where(mask, base, zero) for mask in masks]
+            columns.append(jnp.concatenate(stack, axis=0))
+        left = jnp.concatenate(columns, axis=1)
+        right = jnp.concatenate([one, one, small], axis=1)
+        got = lax.dot_general(left, right, (((1,), (1,)), ((), ())), preferred_element_type=jnp.float32)
         total = got if total is None else total + got
     out_ref[...] += total
 
 
-def read_map(trig, table, pixels, angle_index, flag_mask):
+def cost(samples, cells):
+    return pl.CostEstimate(flops=6 * 3 * samples * cells, bytes_accessed=16 * samples, transcendentals=0)
+
+
+def read_map(trig, table, pixels, angle_index, flag_mask, chunk, chunks):
     n_det, n_samp = pixels.shape
     high = table.shape[0] // 3
-    block = pl.BlockSpec((ROWS, WIDTH), lambda i, j: (i, j))
+    span = n_samp // chunks
+    width = min(max(256, min(WIDTH, WIDTH * 192 // high)), span)
+    steps = span // width
+    block = pl.BlockSpec((ROWS, width), lambda i, j: (i, j + chunk * steps))
     fixed = lambda shape: pl.BlockSpec(shape, lambda i, j: (0, 0))
     return pl.pallas_call(
         functools.partial(read_kernel, high=high),
-        out_shape=jax.ShapeDtypeStruct((n_det, n_samp), jnp.float32),
-        grid=(n_det // ROWS, n_samp // WIDTH),
+        out_shape=jax.ShapeDtypeStruct((n_det, span), jnp.float32),
+        grid=(n_det // ROWS, steps),
         in_specs=[fixed(trig.shape), fixed(table.shape), block, block, block],
-        out_specs=block,
-        scratch_shapes=[pltpu.VMEM((3 * high, 2 * LOW), jnp.bfloat16)],
+        out_specs=pl.BlockSpec((ROWS, width), lambda i, j: (i, j)),
+        scratch_shapes=[pltpu.VMEM((3 * high, 3 * LOW), F8), pltpu.SMEM((1,), jnp.float32)],
         compiler_params=pltpu.CompilerParams(dimension_semantics=("arbitrary", "arbitrary")),
+        cost_estimate=cost(n_det * span, high * LOW),
         name="read_map",
     )(trig, table, pixels, angle_index, flag_mask)
 
 
-def bin_map(trig, pixels, angle_index, flag_mask, values, high):
+def bin_map(trig, pixels, angle_index, flag_mask, values, high, chunk, chunks):
     n_det, n_samp = pixels.shape
-    block = pl.BlockSpec((ROWS, WIDTH), lambda i, j: (i, j))
+    span = n_samp // chunks
+    width = min(max(256, min(WIDTH, WIDTH * 192 // high)), span)
+    steps = span // width
+    scale = scale_of(values).reshape(1)
+    block = pl.BlockSpec((ROWS, width), lambda i, j: (i, j + chunk * steps))
     fixed = lambda shape: pl.BlockSpec(shape, lambda i, j: (0, 0))
-    pieces = pl.pallas_call(
+    binned = pl.pallas_call(
         functools.partial(bin_kernel, high=high),
-        out_shape=jax.ShapeDtypeStruct((6 * high, LOW), jnp.float32),
-        grid=(n_det // ROWS, n_samp // WIDTH),
-        in_specs=[fixed(trig.shape), block, block, block, block],
-        out_specs=fixed((6 * high, LOW)),
+        out_shape=jax.ShapeDtypeStruct((3 * high, LOW), jnp.float32),
+        grid=(n_det // ROWS, steps),
+        in_specs=[
+            fixed(trig.shape),
+            pl.BlockSpec(memory_space=pltpu.SMEM),
+            block,
+            block,
+            block,
+            pl.BlockSpec((ROWS, width), lambda i, j: (i, j)),
+        ],
+        out_specs=fixed((3 * high, LOW)),
         compiler_params=pltpu.CompilerParams(dimension_semantics=("arbitrary", "arbitrary")),
+        cost_estimate=cost(n_det * span, high * LOW),
         name="bin_map",
-    )(trig, pixels, angle_index, flag_mask, values)
-    return pieces[: 3 * high] + pieces[3 * high :]
+    )(trig, scale, pixels, angle_index, flag_mask, values)
+    return binned / scale[0]
 
 
 def mirrored(filt, side_len):
@@ -177,11 +259,26 @@
     high = n_dev * share_len // LOW
     table = jnp.swapaxes(gathered.reshape(n_dev, 3, share_len), 0, 1).reshape(3 * high, LOW)
     trig = jnp.stack([jnp.cos(2.0 * angles), jnp.sin(2.0 * angles)])
-    signal = read_map(trig, table, pixels, angle_index, flag_mask)
-    by_detector = lax.all_to_all(signal, "tm", split_axis=0, concat_axis=1, tiled=True)
+    n_tm = lax.axis_size("tm")
+    n_det, n_samp = pixels.shape
+    chunks = max(1, min(CHUNKS, n_samp // WIDTH))
+    span = n_samp // chunks
+    pieces = []
+    for chunk in range(chunks):
+        signal = read_map(trig, table, pixels, angle_index, flag_mask, chunk, chunks)
+        signal = signal.reshape(n_tm, n_det // n_tm, span)
+        pieces.append(lax.all_to_all(signal, "tm", split_axis=0, concat_axis=0, tiled=True))
+    stacked = jnp.stack(pieces, axis=1)
+    by_detector = jnp.moveaxis(stacked, 2, 0).reshape(n_det // n_tm, n_tm * n_samp)
     filtered = noise_weight(by_detector, inv_noise)
-    returned = lax.all_to_all(filtered, "tm", split_axis=1, concat_axis=0, tiled=True)
-    partial_map = bin_map(trig, pixels, angle_index, flag_mask, returned, high)
+    chunks = min(CHUNKS_BACK, chunks)
+    span = n_samp // chunks
+    parts = jnp.moveaxis(filtered.reshape(n_det // n_tm, n_tm, chunks, span), 0, 2)
+    partial_map = 0.0
+    for chunk in range(chunks):
+        returned = lax.all_to_all(parts[:, chunk], "tm", split_axis=0, concat_axis=0, tiled=True)
+        returned = returned.reshape(n_det, span)
+        partial_map += bin_map(trig, pixels, angle_index, flag_mask, returned, high, chunk, chunks)
     by_owner = jnp.swapaxes(partial_map.reshape(3, n_dev, share_len), 0, 1)
     image = jnp.sum(lax.all_to_all(by_owner, everyone, split_axis=0, concat_axis=0, tiled=True), axis=0)
     scaled_resid = precond * resid_map

time: 527 us -> 426 us (0.81); the launches traced: 527 us -> 419 us
  Pallas kernels: 364 us -> 257 us
  waiting for transfers between devices: 39.3 us -> 27.5 us
    pallas_call x1 -> x2, Pallas kernels: 188 us -> 132 us  [read_map(): pl.pallas_call(functools.partial(read_kernel, high=high), out_shape=jax.S...]
    pallas_call x1, Pallas kernels: 176 us -> 125 us  [bin_map(): pl.pallas_call(functools.partial(bin_kernel, high=high), out_shape=jax.Sh...]
    all_to_all x1 -> x2, waiting for transfers between devices: 20.9 us -> 10.3 us  [body(): lax.all_to_all(signal, 'tm', split_axis=0, concat_axis=0, tiled=True)]
    all_to_all x5 -> x0, local copies, waits for them, and re-layouts: 6.42 us -> none  [the longest x2 4.16 us: body(): lax.all_to_all(signal, 'tm', split_axis=0, concat_axis=1, tiled=True)]
  transfers between devices with their start and end apart: 2 -> 3, of which waited for: 2 -> 2; matrix products, arithmetic and copies ran while one was open for 1% -> 2% of each run, Pallas kernels for 0% -> 16%
where the time goes in v1:
time: 426 us; the launch traced here: 419 us
  Pallas kernels  257 us (60%)
  blocking collectives  61.8 us (15%)
  waiting for transfers between devices  27.5 us (6%)
  matrix products  21.9 us (5%)
  local copies, waits for them, and re-layouts  18.4 us (4%)
  starting transfers between devices  15.8 us (4%)
  other arithmetic  9.02 us (2%)
  between operations  7.16 us (2%)
    pallas_call x2, Pallas kernels, read_map(): pl.pallas_call(functools.partial(read_kernel, high=high), out_shape=jax.S...  132 us
    pallas_call x1, Pallas kernels, bin_map(): pl.pallas_call(functools.partial(bin_kernel, high=high), out_shape=jax.Sh...  125 us
    all_to_all x1, blocking collectives, body(): lax.all_to_all(parts[:, chunk], 'tm', split_axis=0, concat_axis=0, tiled=...  29 us
    all_to_all x1, blocking collectives, body(): lax.all_to_all(by_owner, everyone, split_axis=0, concat_axis=0, tiled=True)  23.6 us
    dot_general x14, matrix products, product(): return jnp.einsum(form, left, right, precision=precision)  21.9 us
    all_to_all x1, waiting for transfers between devices, body(): lax.all_to_all(copies, everyone, split_axis=0, concat_axis=0, tiled=True)  17.1 us
    all_to_all x2, waiting for transfers between devices, body(): lax.all_to_all(signal, 'tm', split_axis=0, concat_axis=0, tiled=True)  10.3 us
    all_to_all x1, blocking collectives, body(): lax.all_to_all(sum_copies, everyone, split_axis=0, concat_axis=0, tiled=T...  9.19 us
  transfers between devices with their start and end apart: 3, of which 2 were waited for; matrix products, arithmetic and copies ran while one was open for 2% of the time, Pallas kernels for 16%

profile of v1, /device:TPU:0, one launch (start us, length us, event | category | flops | bytes accessed | tf_op | source)
XLA Modules:
  0.0 418.7 jit_solution(16769511719480647048)
XLA Ops:
  0.6 0.8 broadcast_in_dim.6
  1.4 0.9 broadcast_in_dim.7
  2.3 7.3 %all-to-all-start = ((f32[32,36,128]{2,1,0:T(8,128)}), f32[32,36,128]{2,1,0:T(8,128)S(1)}, u32[]{:S(2)}, u32[]{:S(2)}) async-start(f32[32,36,128]{2,1,0:T(8,128)} %broadcast_in_dim.7), calls=%async_computation | async-start | bytes 1310720 | tf_op jit(solution)/shard_map/all_to_all | solution.py:258
  9.6 1.3 fusion.102
  11.0 0.6 pad_maximum_fusion.1.trig_ref
  11.5 17.1 %all-to-all-done = f32[32,36,128]{2,1,0:T(8,128)S(1)} async-done(((f32[32,36,128]{2,1,0:T(8,128)}), f32[32,36,128]{2,1,0:T(8,128)S(1)}, u32[]{:S(2)}, u32[]{:S(2)}) %all-to-all-start) | async-done | bytes 589856 | tf_op jit(solution)/shard_map/all_to_all | solution.py:258
  29.1 0.9 reshape.70.table_ref
  30.0 66.0 %read_map.3 = f32[32,4096]{1,0:T(8,128)} custom-call(f32[2,128]{1,0:T(2,128)} %pad_maximum_fusion.1.trig_ref, f32[576,256]{1,0:T(8,128)} %reshape.70.table_ref, s32[32,8192]{1,0:T(8,128)} %pix_ref.5, s32[32,8192]{1,0:T(8,128)} %ang_ref.5, s32[32,8192]{1,0:T(8,128)} %flag_ref.5), custom_call_target="tpu_custom_call" | custom-call | flops 115964116992 | bytes 2097152 | tf_op jit(solution)/shard_map/read_map/pallas_call | solution.py:173
  96.0 2.0 reshape.72
  98.0 3.5 all-to-all-start.2
  101.5 65.9 %read_map.2 = f32[32,4096]{1,0:T(8,128)} custom-call(f32[2,128]{1,0:T(2,128)} %pad_maximum_fusion.1.trig_ref, f32[576,256]{1,0:T(8,128)} %reshape.70.table_ref, s32[32,8192]{1,0:T(8,128)} %pix_ref.5, s32[32,8192]{1,0:T(8,128)} %ang_ref.5, s32[32,8192]{1,0:T(8,128)} %flag_ref.5), custom_call_target="tpu_custom_call" | custom-call | flops 115964116992 | bytes 2097152 | tf_op jit(solution)/shard_map/read_map/pallas_call | solution.py:173
  167.4 2.0 reshape.71
  169.4 5.0 %all-to-all-start.1 = ((f32[8,4,4096]{2,1,0:T(4,128)}), f32[8,4,4096]{2,1,0:T(4,128)S(1)}, u32[]{:S(2)}, u32[]{:S(2)}) async-start(f32[8,4,4096]{2,1,0:T(4,128)} %reshape.71), calls=%async_computation.1 | async-start | bytes 1048576 | tf_op jit(solution)/shard_map/all_to_all | solution.py:270
  174.5 0.5 rev.8
  175.0 0.9 fusion.39
  176.0 0.9 sine_negate_fusion
  177.2 0.9 copy-done
  178.1 0.7 convolution_bitcast_fusion.3
  178.8 0.6 convolution_bitcast_fusion.2
  179.4 10.3 %all-to-all-done.1 = f32[8,4,4096]{2,1,0:T(4,128)S(1)} async-done(((f32[8,4,4096]{2,1,0:T(4,128)}), f32[8,4,4096]{2,1,0:T(4,128)S(1)}, u32[]{:S(2)}, u32[]{:S(2)}) %all-to-all-start.1) | async-done | bytes 524320 | tf_op jit(solution)/shard_map/all_to_all | solution.py:270
  190.0 1.8 copy.109
  191.8 2.1 reshape_reshape.6
  193.9 1.8 convolution_bitcast_fusion
  195.8 1.8 convolution_bitcast_fusion.1
  197.6 1.7 fusion.23
  199.2 1.9 fusion.37
  201.1 1.7 fusion.3
  202.9 1.8 fusion.5
  204.6 1.6 fusion.34
  206.2 1.6 fusion.32
  207.8 1.6 convolution_add_fusion.1
  209.4 1.6 convolution_subtract_fusion
  211.1 1.9 fusion.9
  213.0 1.7 fusion.1
  215.2 0.7 copy.132
  215.9 29.0 %all_to_all.31 = f32[8,4,8192]{2,1,0:T(4,128)S(1)} all-to-all(f32[8,4,8192]{2,1,0:T(4,128)S(1)} %copy.132), channel_id=1, replica_groups=mesh['det'=4,'tm'=8] {'tm'}, dimensions={0} | all-to-all | bytes 2097152 | tf_op jit(solution)/shard_map/all_to_all | solution.py:279
  244.9 1.1 abs_reduce_fusion
  246.7 1.4 reshape.76.val_ref
  248.1 125.2 %bin_map.1 = f32[576,256]{1,0:T(8,128)} custom-call(f32[2,128]{1,0:T(2,128)} %pad_maximum_fusion.1.trig_ref, f32[1]{0:T(128)} %bitcast.24.scale_ref, s32[32,8192]{1,0:T(8,128)} %pix_ref.5, s32[32,8192]{1,0:T(8,128)} %ang_ref.5, s32[32,8192]{1,0:T(8,128)} %flag_ref.5, f32[32,8192]{1,0:T(8,128)} %reshape.76.val_ref), custom_call_target="tpu_custom_call" | custom-call | flops 231928233984 | bytes 4194304 | tf_op jit(solution)/shard_map/bin_map/pallas_call | solution.py:194
  373.3 1.1 broadcast_divide_fusion
  374.6 0.4 copy.171
  375.0 23.6 %all_to_all.32 = f32[32,3,1536]{2,1,0:T(4,128)S(1)} all-to-all(f32[32,3,1536]{2,1,0:T(4,128)S(1)} %bitcast.96), channel_id=1, replica_groups=mesh['det'=4,'tm'=8] {'det','tm'}, dimensions={0} | all-to-all | bytes 1179648 | tf_op jit(solution)/shard_map/all_to_all | solution.py:283
  398.8 0.6 copy-done.3
  399.4 0.6 multiply_reduce_fusion.2
  400.0 2.7 pad_maximum_fusion.2
  402.7 9.2 %all_to_all.33 = f32[32,1,4]{2,1,0:T(1,128)S(1)} all-to-all(f32[32,1,4]{2,1,0:T(1,128)S(1)} %broadcast_in_dim.8), channel_id=1, replica_groups=mesh['det'=4,'tm'=8] {'det','tm'}, dimensions={0} | all-to-all | bytes 1024 | tf_op jit(solution)/shard_map/all_to_all | solution.py:294
  411.9 0.6 fusion.103
  416.5 0.6 multiply_add_fusion.3
  (31 shorter events, 2.1 us)
Async XLA Ops:
  2.3 7.3 %copy-start.2 = (f32[4,32769]{1,0:T(4,128)S(1)}, f32[4,32769]{1,0:T(4,128)}, u32[]{:S(2)}) copy-start(f32[4,32769]{1,0:T(4,128)} %param.17) | copy-start | bytes 1572916
  2.3 26.4 %all-to-all-start = ((f32[32,36,128]{2,1,0:T(8,128)}), f32[32,36,128]{2,1,0:T(8,128)S(1)}, u32[]{:S(2)}, u32[]{:S(2)}) async-start(f32[32,36,128]{2,1,0:T(8,128)} %broadcast_in_dim.7), calls=%async_computation | async-start | bytes 1310720 | tf_op jit(solution)/shard_map/all_to_all | solution.py:258
  9.6 1.3 copy-start.7
  98.0 71.4 %all-to-all-start.2 = ((f32[8,4,4096]{2,1,0:T(4,128)}), f32[8,4,4096]{2,1,0:T(4,128)S(1)}, u32[]{:S(2)}, u32[]{:S(2)}) async-start(f32[8,4,4096]{2,1,0:T(4,128)} %reshape.72), calls=%async_computation.2 | async-start | bytes 1048576 | tf_op jit(solution)/shard_map/all_to_all | solution.py:270
  169.4 20.3 %all-to-all-start.1 = ((f32[8,4,4096]{2,1,0:T(4,128)}), f32[8,4,4096]{2,1,0:T(4,128)S(1)}, u32[]{:S(2)}, u32[]{:S(2)}) async-start(f32[8,4,4096]{2,1,0:T(4,128)} %reshape.71), calls=%async_computation.1 | async-start | bytes 1048576 | tf_op jit(solution)/shard_map/all_to_all | solution.py:270
  176.0 1.0 copy-start.1
  177.1 1.0 copy-start
  398.6 0.7 copy-start.3
  398.6 0.8 copy-start.4
  398.6 0.8 copy-start.5
  411.9 4.6 %copy-start.6 = (f32[3,1536]{1,0:T(4,128)S(1)}, f32[3,1536]{1,0:T(4,128)}, u32[]{:S(2)}) copy-start(f32[3,1536]{1,0:T(4,128)} %param.9) | copy-start | bytes 55300
